TPU v7x, 128 devices: a whole 4x4x4 slice. The times are simulated.
128 devices in a mesh: group: 8 (over y_hi, z), shard: 16 (over x, y_lo, core).
Axes of the slice: x: 4, y: 4 (y_hi: 2, y_lo: 2; y = y_hi * 2 + y_lo), z: 4, core: 2. Of those that a mesh axis runs over, the one named last changes fastest.
Arguments:
- hidden_state: bfloat16 [2048, 8192], P('group', 'shard'), may hold values from -40 to 40
- attn_gain: bfloat16 [8192], replicated, may hold values from 0.5 to 1.5
- ffn_gain: bfloat16 [8192], replicated, may hold values from 0.5 to 1.5
- w_query: bfloat16 [8192, 8192], P('group', 'shard'), may hold values from -0.125 to 0.125
- w_keyval: bfloat16 [8192, 2048], P('group', 'shard'), may hold values from -0.0625 to 0.0625
- w_output: bfloat16 [8192, 8192], P('shard', 'group'), may hold values from -0.0625 to 0.0625
- cache_keys: bfloat16 [2048, 8, 192, 128], P(('group', 'shard')), may hold values from -256 to 256
- cache_values: bfloat16 [2048, 8, 192, 128], P(('group', 'shard')), may hold values from -6 to 6
- lengths: int32 [2048], P('group'), may hold values from 2 to 192, as said below
Outputs:
- branch: bfloat16 [2048, 8192], P('group', 'shard')
- ffn_input: bfloat16 [2048, 8192], P('group', 'shard')
Inputs may be any that keep to these rules, and one draw needn't show every extreme that they name: `lengths`: in every aligned block of 16 sequences, at least one has all 192 cached positions live.
All inputs are finite; a program needn't handle non-finite values.
Results may differ from a plain program's by a relative error of at most 0.012.
The roundings to bfloat16 on the way count: a program that leaves them out, or rounds other values in their place, can miss the bound.
Values may be sent and summed in bfloat16 or wider, within the bound.
No kernel may reach another device: no remote copies, remote signals or barrier semaphores. Data moves between devices by JAX's collectives and lax.ppermute only.
A program may use at most 128 MiB of HBM per device.

v0:
```python
import jax
import jax.numpy as jnp
from jax import lax
from jax.sharding import PartitionSpec as P

epsilon = 1e-05
rope_base = 500000.0


def sent_together(arrays, axis, dim, along):
    both = jnp.concatenate(arrays, axis=along)
    filled, at, gathered = (lax.all_gather(both, axis, axis=dim, tiled=True), 0, [])
    for a in arrays:
        gathered.append(lax.slice_in_dim(filled, at, at + a.shape[along], axis=along))
        at += a.shape[along]
    return tuple(gathered)


def from_everyone(x, axis):
    devices = lax.axis_size(axis)
    return lax.all_to_all(jnp.broadcast_to(x[None], (devices, *x.shape)), axis, 0, 0, tiled=True)


def over_copies(x, axis):
    everything = from_everyone(x, axis)
    return jnp.sum(everything, axis=0)


def rotate(heads_block, position):
    head_dim = heads_block.shape[-1]
    half_dim = head_dim // 2
    frequency = rope_base ** (-2.0 * jnp.arange(half_dim, dtype=jnp.float32) / head_dim)
    angles = position.astype(jnp.float32)[:, None] * frequency[None, :]
    cosine = jnp.cos(angles)[:, None, :]
    sine_part = jnp.sin(angles)[:, None, :]
    lower_half = heads_block[..., :half_dim]
    upper_half = heads_block[..., half_dim:]
    return jnp.concatenate(
        [
            lower_half * cosine - upper_half * sine_part,
            upper_half * cosine + lower_half * sine_part,
        ],
        axis=-1,
    )


def attend(queries, fresh, cache_keys, cache_values, lengths):
    seq_count, kv_heads, cache_len, head_dim = cache_keys.shape
    q_heads = queries.shape[1] // head_dim
    q_per_kv = q_heads // kv_heads
    kv_width = kv_heads * head_dim
    grouped = queries.reshape(seq_count, kv_heads, q_per_kv, head_dim)
    new_keys = fresh[:, :kv_width].reshape(seq_count, kv_heads, head_dim)
    new_values = fresh[:, kv_width:].reshape(seq_count, kv_heads, head_dim)
    score_scale = head_dim ** (-0.5)
    scores = (
        jnp.einsum("nkgd,nkld->nkgl", grouped, cache_keys, preferred_element_type=jnp.float32)
        * score_scale
    )
    self_score = (
        jnp.einsum("nkgd,nkd->nkg", grouped, new_keys, preferred_element_type=jnp.float32)
        * score_scale
    )
    live_mask = jnp.arange(cache_len, dtype=jnp.int32)[None, :] < lengths[:, None]
    scores = jnp.where(live_mask[:, None, None, :], scores, -1e30)
    row_top = jnp.maximum(jnp.max(scores, axis=3), self_score)
    exp_scores = jnp.exp(scores - row_top[..., None])
    self_weight = jnp.exp(self_score - row_top)
    denom_sum = jnp.sum(exp_scores, axis=3) + self_weight
    weight_bf = (exp_scores / denom_sum[..., None]).astype(jnp.bfloat16)
    self_bf = (self_weight / denom_sum).astype(jnp.bfloat16)
    context = jnp.einsum(
        "nkgl,nkld->nkgd", weight_bf, cache_values, preferred_element_type=jnp.float32
    )
    context = (
        context
        + self_bf.astype(jnp.float32)[..., None] * new_values.astype(jnp.float32)[:, :, None, :]
    )
    return context.reshape(seq_count, q_heads * head_dim).astype(jnp.bfloat16)


def local(
    hidden_state,
    attn_gain,
    ffn_gain,
    w_query,
    w_keyval,
    w_output,
    cache_keys,
    cache_values,
    lengths,
):
    token_count, local_width = hidden_state.shape
    shard_count = lax.axis_size("shard")
    shard_pos = lax.axis_index("shard")
    model_width = local_width * shard_count
    col_start = shard_pos * local_width
    resident = hidden_state.astype(jnp.float32)
    attn_scale = attn_gain.astype(jnp.float32)
    whole_rows = lax.all_gather(hidden_state, "shard", axis=1, tiled=True).astype(jnp.float32)
    inverse = lax.rsqrt(jnp.mean(whole_rows * whole_rows, axis=1, keepdims=True) + epsilon)
    normed = (whole_rows * inverse * attn_scale).astype(jnp.bfloat16)
    pieces = sent_together((w_query, w_keyval), "group", 0, 1)
    queries = jnp.dot(normed, pieces[0], preferred_element_type=jnp.float32)
    keyval = jnp.dot(normed, pieces[1], preferred_element_type=jnp.float32)
    head_dim = cache_keys.shape[3]
    q_cols = queries.shape[1]
    kv_cols = keyval.shape[1]
    roped_q = (
        rotate(queries.reshape(token_count, q_cols // head_dim, head_dim), lengths)
        .reshape(token_count, q_cols)
        .astype(jnp.bfloat16)
    )
    turned = rotate(keyval.reshape(token_count, kv_cols // head_dim, head_dim), lengths).reshape(
        token_count, kv_cols
    )
    key_side = shard_pos * kv_cols < kv_cols * shard_count // 2
    fresh = jnp.where(key_side, turned, keyval).astype(jnp.bfloat16)
    owner_q, owner_kv = (
        lax.all_to_all(roped_q, "shard", split_axis=0, concat_axis=1, tiled=True),
        lax.all_to_all(fresh, "shard", split_axis=0, concat_axis=1, tiled=True),
    )
    seq_dev = cache_keys.shape[0]
    owner_len = lax.dynamic_slice_in_dim(lengths, shard_pos * seq_dev, seq_dev)
    context = attend(owner_q, owner_kv, cache_keys, cache_values, owner_len)
    back_rows = lax.all_to_all(context, "shard", split_axis=1, concat_axis=0, tiled=True)
    partial_value = jnp.dot(
        back_rows,
        lax.all_gather(w_output, "group", axis=1, tiled=True),
        preferred_element_type=jnp.float32,
    )
    summed = lax.psum_scatter(partial_value, "shard", scatter_dimension=1, tiled=True)
    ffn_scale = lax.dynamic_slice_in_dim(ffn_gain.astype(jnp.float32), col_start, local_width)
    stream = resident + summed
    branch = summed.astype(jnp.bfloat16)
    squares_two = over_copies(jnp.sum(stream * stream, axis=1), "shard")
    inverse_two = lax.rsqrt(squares_two / model_width + epsilon)[:, None]
    ffn_input = (stream * inverse_two * ffn_scale).astype(jnp.bfloat16)
    return (branch, ffn_input)


def solution(mesh):
    placed = (
        P("group", "shard"),
        P(),
        P(),
        P("group", "shard"),
        P("group", "shard"),
        P("shard", "group"),
        P(("group", "shard"), None, None, None),
        P(("group", "shard"), None, None, None),
        P("group"),
    )
    return jax.shard_map(
        local,
        mesh=mesh,
        in_specs=placed,
        out_specs=(P("group", "shard"), P("group", "shard")),
        check_vma=False,
    )
```

profile of v0, /device:TPU:1, one launch (start us, length us, event | category | flops | bytes accessed | tf_op | source)
XLA Modules:
  0.0 413.2 jit_solution(4423881980820156677)
XLA Ops:
  7.2 0.0 all-gather.4.cloned.1.call-start
  7.2 0.7 all-gather.4.cloned.1.call-update
  7.9 0.0 all-gather.6.cloned.1.call-start
  7.9 2.5 pad_maximum_fusion
  10.4 0.0 all-gather.6.cloned.1.call-update
  10.5 0.0 all-gather.8.cloned.1.call-start
  10.5 0.7 all-gather.8.cloned.1.call-update
  11.2 0.7 convert_element_type.60
  11.9 0.7 convert_element_type.62
  12.6 0.8 dynamic_slice.6
  13.4 0.1 iota_compare_fusion
  13.4 0.5 multiply_cosine_fusion
  14.0 36.4 %all-gather.4.cloned.1.call-done = bf16[256,8192]{1,0:T(8,128)(2,1)} async-done(((bf16[256,512]{1,0:T(8,128)(2,1)}), bf16[256,8192]{1,0:T(8,128)(2,1)}) %all-gather.4.cloned.1.call-update) | async-done | bytes 4194320 | tf_op jit(solution)/shard_map/all_gather | solution.py:100
  50.3 3.1 fusion
  53.5 123.9 %all-gather.6.cloned.1.call-done = bf16[8192,640]{1,0:T(8,128)(2,1)} async-done(((bf16[1024,640]{1,0:T(8,128)(2,1)}), bf16[8192,640]{1,0:T(8,128)(2,1)}) %all-gather.6.cloned.1.call-update) | async-done | bytes 10485776 | tf_op jit(solution)/shard_map/all_gather | solution.py:12
  177.4 4.6 %fusion.5 = f32[256,128]{0,1:T(8,128)S(1)} fusion(bf16[8192,640]{1,0:T(8,128)(2,1)} %all-gather.6.cloned.1.call-done, bf16[256,8192]{1,0:T(8,128)(2,1)} %all-gather.4.cloned.1.call-done, f32[8192]{0:T(1024)S(1)} %convert_element_type.60, f32[256]{0:T(256)S(1)} %add_rsqrt_fusion.1), kind=kOutput, calls=%fused_computation.7 | convolution fusion | flops 545259520 | bytes 6456320 | tf_op jit(solution)/shard_map/dot_general | solution.py:105
  182.0 0.3 fusion.20
  182.3 0.7 copy.25
  183.1 5.7 %all-to-all-start.1 = ((bf16[16,16,128]{2,1,0:T(8,128)(2,1)}), bf16[16,16,128]{2,1,0:T(8,128)(2,1)S(1)}, u32[]{:S(2)}, u32[]{:S(2)}) async-start(bf16[16,16,128]{2,1,0:T(8,128)(2,1)} %bitcast.3), calls=%async_computation.1 | async-start | bytes 131072 | tf_op jit(solution)/shard_map/all_to_all | solution.py:121
  188.7 7.5 %fusion.3 = f32[256,512]{1,0:T(8,128)S(1)} fusion(bf16[8192,640]{1,0:T(8,128)(2,1)} %all-gather.6.cloned.1.call-done, bf16[256,8192]{1,0:T(8,128)(2,1)} %all-gather.4.cloned.1.call-done, f32[8192]{0:T(1024)S(1)} %convert_element_type.60, f32[256]{0:T(256)S(1)} %add_rsqrt_fusion.1), kind=kOutput, calls=%fused_computation.5 | convolution fusion | flops 2155872256 | bytes 13140992 | tf_op jit(solution)/shard_map/dot_general | solution.py:104
  196.2 0.2 reshape.180
  196.4 0.5 subtract_convert_fusion
  196.9 0.4 pad_maximum_fusion.1
  197.3 0.8 convert_element_type.63
  198.1 0.0 all-to-all-done.1
  198.1 5.7 %all-to-all-start = ((bf16[16,16,512]{2,1,0:T(8,128)(2,1)}), bf16[16,16,512]{2,1,0:T(8,128)(2,1)S(1)}, u32[]{:S(2)}, u32[]{:S(2)}) async-start(bf16[16,16,512]{2,1,0:T(8,128)(2,1)} %convert_element_type.63), calls=%async_computation | async-start | bytes 524288 | tf_op jit(solution)/shard_map/all_to_all | solution.py:120
  203.9 7.3 %all-to-all-done = bf16[16,16,512]{2,1,0:T(8,128)(2,1)S(1)} async-done(((bf16[16,16,512]{2,1,0:T(8,128)(2,1)}), bf16[16,16,512]{2,1,0:T(8,128)(2,1)S(1)}, u32[]{:S(2)}, u32[]{:S(2)}) %all-to-all-start) | async-done | bytes 262176 | tf_op jit(solution)/shard_map/all_to_all | solution.py:120
  211.2 0.1 copy.24
  211.3 0.2 reshape.181
  211.5 0.3 fusion.25
  211.8 6.2 %fusion.24 = (f32[16,8,8]{2,1,0:T(8,128)S(1)}, f32[16,8,8,192]{3,2,1,0:T(8,128)S(1)}) fusion(bf16[16,8,8,128]{3,2,1,0:T(8,128)(2,1)S(1)} %reshape.181, bf16[16,8,192,128]{3,2,1,0:T(8,128)(2,1)} %param.15, pred[16,192]{1,0:T(8,128)(4,1)S(1)} %iota_compare_fusion), kind=kOutput, calls=%fused_computation.50 | convolution fusion | flops 50920448 | bytes 7347200 | tf_op jit(solution)/shard_map/nkgd,nkld->nkgl/dot_general | solution.py:57
  218.0 0.4 fusion.11
  218.5 4.6 %fusion.8 = bf16[16,8,8,128]{3,2,1,0:T(8,128)(2,1)S(1)} fusion(bf16[16,8,192,128]{3,2,1,0:T(8,128)(2,1)} %param.16, f32[16,8,8,192]{3,2,1,0:T(8,128)S(1)} %get-tuple-element.15, f32[16,8,8]{2,1,0:T(8,128)S(1)} %get-tuple-element.7, f32[16,8,8]{2,1,0:T(8,128)S(1)} %multiply_maximum_fusion, f32[16,8,128]{2,1,0:T(8,128)S(1)} %bitcast.37, ...), kind=kOutput, calls=%fused_computation.13 | convolution fusion | flops 51314688 | bytes 7417856 | tf_op jit(solution)/shard_map/nkgl,nkld->nkgd/dot_general | solution.py:72
  223.1 0.2 convert_element_type.71
  223.3 0.9 copy.27
  224.1 3.9 all-to-all-start.2
  228.0 0.0 reduce-scatter.2.cloned.1.call-start
  228.0 58.9 %all-gather.8.cloned.1.call-done = bf16[512,8192]{1,0:T(8,128)(2,1)} async-done(((bf16[512,1024]{1,0:T(8,128)(2,1)}), bf16[512,8192]{1,0:T(8,128)(2,1)}) %all-gather.8.cloned.1.call-update) | async-done | bytes 8388624 | tf_op jit(solution)/shard_map/all_gather | solution.py:129
  287.0 0.0 all-to-all-done.2
  287.0 9.0 %fusion.26 = f32[256,8192]{1,0:T(8,128)} fusion(bf16[256,512]{1,0:T(8,128)(2,1)S(1)} %bitcast.32, bf16[512,8192]{1,0:T(8,128)(2,1)} %all-gather.8.cloned.1.call-done), kind=kOutput, calls=%fused_computation.52 | convolution fusion | flops 2147483648 | bytes 17039360 | tf_op jit(solution)/shard_map/dot_general | solution.py:127
  295.9 0.0 copy-start
  295.9 0.0 reduce-scatter.2.cloned.1.call-update
  295.9 95.3 %reduce-scatter.2.cloned.1.call-done = f32[256,512]{1,0:T(8,128)} async-done(((f32[256,8192]{1,0:T(8,128)}), f32[256,512]{1,0:T(8,128)}) %reduce-scatter.2.cloned.1.call-update) | async-done | bytes 524304 | tf_op jit(solution)/shard_map/reduce_scatter | solution.py:132
  391.3 0.0 copy-done
  391.3 1.2 multiply_reduce_fusion
  392.5 0.6 broadcast_in_dim.12
  393.1 5.7 %all-to-all-start.3 = ((f32[16,1,256]{2,1,0:T(1,128)}), f32[16,1,256]{2,1,0:T(1,128)S(1)}, u32[]{:S(2)}, u32[]{:S(2)}) async-start(f32[16,1,256]{2,1,0:T(1,128)} %broadcast_in_dim.12), calls=%async_computation.4 | async-start | bytes 32768 | tf_op jit(solution)/shard_map/all_to_all | solution.py:21
  398.8 0.8 dynamic-slice_convert_fusion
  399.5 5.0 %all-to-all-done.3 = f32[16,1,256]{2,1,0:T(1,128)S(1)} async-done(((f32[16,1,256]{2,1,0:T(1,128)}), f32[16,1,256]{2,1,0:T(1,128)S(1)}, u32[]{:S(2)}, u32[]{:S(2)}) %all-to-all-start.3) | async-done | bytes 16416 | tf_op jit(solution)/shard_map/all_to_all | solution.py:21
  404.6 2.1 multiply_convert_fusion
  (11 shorter events, 0.2 us)
Async XLA Ops:
  7.2 43.2 %all-gather.4.cloned.1.call-start = ((), (), s32[]{:S(2)}) async-start(), calls=%async_computation.5 | async-start | bytes 4456448 | tf_op jit(solution)/shard_map/all_gather | solution.py:100
  7.9 169.5 %all-gather.6.cloned.1.call-start = ((), (), s32[]{:S(2)}) async-start(), calls=%async_computation.6 | async-start | bytes 11796480 | tf_op jit(solution)/shard_map/all_gather | solution.py:12
  10.5 276.5 %all-gather.8.cloned.1.call-start = ((), (), s32[]{:S(2)}) async-start(), calls=%async_computation.7 | async-start | bytes 9437184 | tf_op jit(solution)/shard_map/all_gather | solution.py:129
  183.1 15.0 %all-to-all-start.1 = ((bf16[16,16,128]{2,1,0:T(8,128)(2,1)}), bf16[16,16,128]{2,1,0:T(8,128)(2,1)S(1)}, u32[]{:S(2)}, u32[]{:S(2)}) async-start(bf16[16,16,128]{2,1,0:T(8,128)(2,1)} %bitcast.3), calls=%async_computation.1 | async-start | bytes 131072 | tf_op jit(solution)/shard_map/all_to_all | solution.py:121
  198.1 13.1 %all-to-all-start = ((bf16[16,16,512]{2,1,0:T(8,128)(2,1)}), bf16[16,16,512]{2,1,0:T(8,128)(2,1)S(1)}, u32[]{:S(2)}, u32[]{:S(2)}) async-start(bf16[16,16,512]{2,1,0:T(8,128)(2,1)} %convert_element_type.63), calls=%async_computation | async-start | bytes 524288 | tf_op jit(solution)/shard_map/all_to_all | solution.py:120
  224.1 62.9 %all-to-all-start.2 = ((bf16[16,16,512]{2,0,1:T(8,128)(2,1)}), bf16[16,16,512]{2,0,1:T(8,128)(2,1)S(1)}, u32[]{:S(2)}, u32[]{:S(2)}) async-start(bf16[16,16,512]{2,0,1:T(8,128)(2,1)} %copy.27), calls=%async_computation.2 | async-start | bytes 524288 | tf_op jit(solution)/shard_map/all_to_all | solution.py:126
  228.0 163.3 %reduce-scatter.2.cloned.1.call-start = ((), (), s32[]{:S(2)}) async-start(), calls=%async_computation.8 | async-start | bytes 8912896 | tf_op jit(solution)/shard_map/reduce_scatter | solution.py:132
  295.9 95.4 %copy-start = (bf16[256,512]{1,0:T(8,128)(2,1)S(1)}, bf16[256,512]{1,0:T(8,128)(2,1)}, u32[]{:S(2)}) copy-start(bf16[256,512]{1,0:T(8,128)(2,1)} %param.9) | copy-start | bytes 786436
  393.1 11.5 %all-to-all-start.3 = ((f32[16,1,256]{2,1,0:T(1,128)}), f32[16,1,256]{2,1,0:T(1,128)S(1)}, u32[]{:S(2)}, u32[]{:S(2)}) async-start(f32[16,1,256]{2,1,0:T(1,128)} %broadcast_in_dim.12), calls=%async_computation.4 | async-start | bytes 32768 | tf_op jit(solution)/shard_map/all_to_all | solution.py:21
Sparse Core Ops, SparseCore 0:
  9.6 40.6 all-gather.3
  52.6 124.6 all-gather.5
  179.7 107.2 all-gather.7
  296.1 95.1 reduce-scatter.1
where the time goes:
time: 414 us; the launch traced here: 413 us
  waiting for transfers between devices  328 us (79%)
  matrix products  32.1 us (8%)
  starting transfers between devices  21.2 us (5%)
  between operations  13.9 us (3%)
  other arithmetic  13.4 us (3%)
  local copies, waits for them, and re-layouts  4.48 us (1%)
    all_gather x1, waiting for transfers between devices, sent_together(): lax.all_gather(both, axis, axis=dim, tiled=True)  124 us
    reduce_scatter x1, waiting for transfers between devices, local(): lax.psum_scatter(partial_value, 'shard', scatter_dimension=1, tiled=True)  95.3 us
    all_gather x1, waiting for transfers between devices, local(): lax.all_gather(w_output, 'group', axis=1, tiled=True)  58.9 us
    all_gather x1, waiting for transfers between devices, local(): lax.all_gather(hidden_state, 'shard', axis=1, tiled=True)  36.4 us
    dot_general x1, matrix products, local(): jnp.dot(back_rows, lax.all_gather(w_output, 'group', axis=1, tiled=True),...  8.95 us
  transfers between devices with their start and end apart: 8, of which 6 were waited for; matrix products, arithmetic and copies ran while one was open for 9% of the time, Pallas kernels for 0%

commit v1 on v0

--- a/solution.py
+++ b/solution.py
@@ -126,7 +126,9 @@
     back_rows = lax.all_to_all(context, "shard", split_axis=1, concat_axis=0, tiled=True)
     partial_value = jnp.dot(
         back_rows,
-        lax.all_gather(w_output, "group", axis=1, tiled=True),
+        jnp.concatenate(
+            lax.all_to_all(jnp.stack([w_output] * lax.axis_size("group")), "group", 0, 0), axis=1
+        ),
         preferred_element_type=jnp.float32,
     )
     summed = lax.psum_scatter(partial_value, "shard", scatter_dimension=1, tiled=True)

time: 414 us -> 451 us (1.089)
  waiting for transfers between devices: 328 us -> 350 us
  blocking collectives: 0 us -> 11.1 us
    all_to_all x1, waiting for transfers between devices: 0.01 us -> 80.9 us  [local(): lax.all_to_all(jnp.stack([w_output] * lax.axis_size('group')), 'group', 0...]
    all_gather x1 -> x0, waiting for transfers between devices: 58.9 us -> none  [local(): lax.all_gather(w_output, 'group', axis=1, tiled=True)]
    all_to_all x0 -> x1, blocking collectives: none -> 11.1 us  [local(): lax.all_to_all(context, 'shard', split_axis=1, concat_axis=0, tiled=True)]
  transfers between devices with their start and end apart: 8 -> 7, of which waited for: 6 -> 6; matrix products, arithmetic and copies ran while one was open for 9% -> 7% of each run, Pallas kernels for 0% -> 0%
where the time goes in v1:
time: 451 us; the launch traced here: 450 us
  waiting for transfers between devices  350 us (78%)
  matrix products  31.9 us (7%)
  starting transfers between devices  22.1 us (5%)
  between operations  13.9 us (3%)
  other arithmetic  13.4 us (3%)
  blocking collectives  11.1 us (2%)
  local copies, waits for them, and re-layouts  7.6 us (2%)
    all_gather x1, waiting for transfers between devices, sent_together(): lax.all_gather(both, axis, axis=dim, tiled=True)  124 us
    reduce_scatter x1, waiting for transfers between devices, local(): lax.psum_scatter(partial_value, 'shard', scatter_dimension=1, tiled=True)  95 us
    all_to_all x1, waiting for transfers between devices, local(): lax.all_to_all(jnp.stack([w_output] * lax.axis_size('group')), 'group', 0...  80.9 us
    all_gather x1, waiting for transfers between devices, local(): lax.all_gather(hidden_state, 'shard', axis=1, tiled=True)  37.9 us
    all_to_all x1, blocking collectives, local(): lax.all_to_all(context, 'shard', split_axis=1, concat_axis=0, tiled=True)  11.1 us
    dot_general x1, matrix products, local(): jnp.dot(back_rows, jnp.concatenate(lax.all_to_all(jnp.stack([w_output] *...  9.11 us
  transfers between devices with their start and end apart: 7, of which 6 were waited for; matrix products, arithmetic and copies ran while one was open for 7% of the time, Pallas kernels for 0%

profile of v1, /device:TPU:1, one launch (start us, length us, event | category | flops | bytes accessed | tf_op | source)
XLA Modules:
  0.0 450.4 jit_solution(2764077932932250490)
XLA Ops:
  7.2 0.0 all-gather.3.cloned.1.call-start
  7.2 0.7 all-gather.3.cloned.1.call-update
  7.9 0.0 all-gather.5.cloned.1.call-start
  7.9 2.5 pad_maximum_fusion
  10.5 0.0 all-gather.5.cloned.1.call-update
  10.5 0.7 convert_element_type.60
  11.2 0.7 convert_element_type.62
  11.9 0.5 multiply_cosine_fusion
  12.5 37.9 %all-gather.3.cloned.1.call-done = bf16[256,8192]{1,0:T(8,128)(2,1)} async-done(((bf16[256,512]{1,0:T(8,128)(2,1)}), bf16[256,8192]{1,0:T(8,128)(2,1)}) %all-gather.3.cloned.1.call-update) | async-done | bytes 4194320 | tf_op jit(solution)/shard_map/all_gather | solution.py:100
  50.3 3.1 fusion
  53.5 123.9 %all-gather.5.cloned.1.call-done = bf16[8192,640]{1,0:T(8,128)(2,1)} async-done(((bf16[1024,640]{1,0:T(8,128)(2,1)}), bf16[8192,640]{1,0:T(8,128)(2,1)}) %all-gather.5.cloned.1.call-update) | async-done | bytes 10485776 | tf_op jit(solution)/shard_map/all_gather | solution.py:12
  177.4 4.6 %fusion.5 = f32[256,128]{0,1:T(8,128)S(1)} fusion(bf16[8192,640]{1,0:T(8,128)(2,1)} %all-gather.5.cloned.1.call-done, bf16[256,8192]{1,0:T(8,128)(2,1)} %all-gather.3.cloned.1.call-done, f32[8192]{0:T(1024)S(1)} %convert_element_type.60, f32[256]{0:T(256)S(1)} %add_rsqrt_fusion.1), kind=kOutput, calls=%fused_computation.7 | convolution fusion | flops 545259520 | bytes 6456320 | tf_op jit(solution)/shard_map/dot_general | solution.py:105
  182.0 0.3 fusion.20
  182.3 0.7 copy.28
  183.1 5.7 %all-to-all-start.1 = ((bf16[16,16,128]{2,1,0:T(8,128)(2,1)}), bf16[16,16,128]{2,1,0:T(8,128)(2,1)S(1)}, u32[]{:S(2)}, u32[]{:S(2)}) async-start(bf16[16,16,128]{2,1,0:T(8,128)(2,1)} %bitcast.3), calls=%async_computation.1 | async-start | bytes 131072 | tf_op jit(solution)/shard_map/all_to_all | solution.py:121
  188.7 0.0 copy-start.1
  188.8 7.1 %fusion.3 = f32[256,512]{1,0:T(8,128)S(1)} fusion(bf16[8192,640]{1,0:T(8,128)(2,1)} %all-gather.5.cloned.1.call-done, bf16[256,8192]{1,0:T(8,128)(2,1)} %all-gather.3.cloned.1.call-done, f32[8192]{0:T(1024)S(1)} %convert_element_type.60, f32[256]{0:T(256)S(1)} %add_rsqrt_fusion.1), kind=kOutput, calls=%fused_computation.5 | convolution fusion | flops 2155872256 | bytes 13140992 | tf_op jit(solution)/shard_map/dot_general | solution.py:104
  195.9 0.2 reshape.188
  196.1 0.5 subtract_convert_fusion
  196.5 0.4 pad_maximum_fusion.1
  196.9 0.8 convert_element_type.63
  197.7 0.0 all-to-all-done.1
  197.7 5.7 %all-to-all-start = ((bf16[16,16,512]{2,1,0:T(8,128)(2,1)}), bf16[16,16,512]{2,1,0:T(8,128)(2,1)S(1)}, u32[]{:S(2)}, u32[]{:S(2)}) async-start(bf16[16,16,512]{2,1,0:T(8,128)(2,1)} %convert_element_type.63), calls=%async_computation | async-start | bytes 524288 | tf_op jit(solution)/shard_map/all_to_all | solution.py:120
  203.4 0.0 copy-done.1
  203.4 0.5 copy.31
  204.0 6.8 %all-to-all-done = bf16[16,16,512]{2,1,0:T(8,128)(2,1)S(1)} async-done(((bf16[16,16,512]{2,1,0:T(8,128)(2,1)}), bf16[16,16,512]{2,1,0:T(8,128)(2,1)S(1)}, u32[]{:S(2)}, u32[]{:S(2)}) %all-to-all-start) | async-done | bytes 262176 | tf_op jit(solution)/shard_map/all_to_all | solution.py:120
  210.8 4.0 stack.2
  214.7 0.0 copy-start.2
  214.7 5.1 %all-to-all-start.3 = ((bf16[8,512,1024]{1,2,0:T(8,128)(2,1)}), bf16[8,512,1024]{1,2,0:T(8,128)(2,1)}, u32[]{:S(2)}, u32[]{:S(2)}) async-start(bf16[8,512,1024]{1,2,0:T(8,128)(2,1)} %stack.2), calls=%async_computation.3 | async-start | bytes 16777216 | tf_op jit(solution)/shard_map/all_to_all | solution.py:130
  219.8 0.2 reduce-scatter.2.cloned.1.call-start
  220.1 0.0 copy-done.2
  220.1 0.1 dynamic_slice.6
  220.1 0.1 iota_compare_fusion
  220.3 0.2 copy.27
  220.5 0.2 reshape.189
  220.6 0.3 fusion.25
  220.9 6.2 %fusion.24 = (f32[16,8,8]{2,1,0:T(8,128)S(1)}, f32[16,8,8,192]{3,2,1,0:T(8,128)S(1)}) fusion(bf16[16,8,8,128]{3,2,1,0:T(8,128)(2,1)S(1)} %reshape.189, bf16[16,8,192,128]{3,2,1,0:T(8,128)(2,1)} %param.15, pred[16,192]{1,0:T(8,128)(4,1)S(1)} %iota_compare_fusion), kind=kOutput, calls=%fused_computation.50 | convolution fusion | flops 50920448 | bytes 7347200 | tf_op jit(solution)/shard_map/nkgd,nkld->nkgl/dot_general | solution.py:57
  227.2 0.4 fusion.11
  227.6 4.6 %fusion.8 = bf16[16,8,8,128]{3,2,1,0:T(8,128)(2,1)S(1)} fusion(bf16[16,8,192,128]{3,2,1,0:T(8,128)(2,1)} %param.16, f32[16,8,8,192]{3,2,1,0:T(8,128)S(1)} %get-tuple-element.15, f32[16,8,8]{2,1,0:T(8,128)S(1)} %get-tuple-element.7, f32[16,8,8]{2,1,0:T(8,128)S(1)} %multiply_maximum_fusion, f32[16,8,128]{2,1,0:T(8,128)S(1)} %bitcast.40, ...), kind=kOutput, calls=%fused_computation.13 | convolution fusion | flops 51314688 | bytes 7417856 | tf_op jit(solution)/shard_map/nkgl,nkld->nkgd/dot_general | solution.py:72
  232.2 0.2 convert_element_type.71
  232.4 0.2 copy.30
  232.6 80.9 %all-to-all-done.3 = bf16[8,512,1024]{1,2,0:T(8,128)(2,1)} async-done(((bf16[8,512,1024]{1,2,0:T(8,128)(2,1)}), bf16[8,512,1024]{1,2,0:T(8,128)(2,1)}, u32[]{:S(2)}, u32[]{:S(2)}) %all-to-all-start.3) | async-done | bytes 8388640 | tf_op jit(solution)/shard_map/all_to_all | solution.py:130
  313.4 11.1 %all_to_all.59 = bf16[16,16,512]{2,0,1:T(8,128)(2,1)S(1)} all-to-all(bf16[16,16,512]{2,0,1:T(8,128)(2,1)S(1)} %copy.30), channel_id=1, replica_groups=mesh['group'=8,'shard'=16] {'shard'}, dimensions={1} | all-to-all | bytes 524288 | tf_op jit(solution)/shard_map/all_to_all | solution.py:126
  324.6 9.1 %fusion.26 = f32[256,8192]{1,0:T(8,128)} fusion(bf16[256,512]{1,0:T(8,128)(2,1)S(1)} %bitcast.35, bf16[512,8192]{0,1:T(8,128)(2,1)} %bitcast.10), kind=kOutput, calls=%fused_computation.52 | convolution fusion | flops 2147483648 | bytes 17039360 | tf_op jit(solution)/shard_map/dot_general | solution.py:127
  333.7 0.0 copy-start
  333.7 0.0 reduce-scatter.2.cloned.1.call-update
  333.7 95.0 %reduce-scatter.2.cloned.1.call-done = f32[256,512]{1,0:T(8,128)} async-done(((f32[256,8192]{1,0:T(8,128)}), f32[256,512]{1,0:T(8,128)}) %reduce-scatter.2.cloned.1.call-update) | async-done | bytes 524304 | tf_op jit(solution)/shard_map/reduce_scatter | solution.py:134
  428.7 0.0 copy-done
  428.7 1.2 multiply_reduce_fusion
  429.9 0.6 broadcast_in_dim.12
  430.5 5.4 %all-to-all-start.4 = ((f32[16,1,256]{2,1,0:T(1,128)}), f32[16,1,256]{2,1,0:T(1,128)S(1)}, u32[]{:S(2)}, u32[]{:S(2)}) async-start(f32[16,1,256]{2,1,0:T(1,128)} %broadcast_in_dim.12), calls=%async_computation.5 | async-start | bytes 32768 | tf_op jit(solution)/shard_map/all_to_all | solution.py:21
  435.9 0.8 dynamic-slice_convert_fusion
  436.7 5.0 %all-to-all-done.4 = f32[16,1,256]{2,1,0:T(1,128)S(1)} async-done(((f32[16,1,256]{2,1,0:T(1,128)}), f32[16,1,256]{2,1,0:T(1,128)S(1)}, u32[]{:S(2)}, u32[]{:S(2)}) %all-to-all-start.4) | async-done | bytes 16416 | tf_op jit(solution)/shard_map/all_to_all | solution.py:21
  441.7 2.1 multiply_convert_fusion
  (11 shorter events, 0.2 us)
Async XLA Ops:
  7.2 43.2 %all-gather.3.cloned.1.call-start = ((), (), s32[]{:S(2)}) async-start(), calls=%async_computation.6 | async-start | bytes 4456448 | tf_op jit(solution)/shard_map/all_gather | solution.py:100
  7.9 169.5 %all-gather.5.cloned.1.call-start = ((), (), s32[]{:S(2)}) async-start(), calls=%async_computation.7 | async-start | bytes 11796480 | tf_op jit(solution)/shard_map/all_gather | solution.py:12
  183.1 14.7 %all-to-all-start.1 = ((bf16[16,16,128]{2,1,0:T(8,128)(2,1)}), bf16[16,16,128]{2,1,0:T(8,128)(2,1)S(1)}, u32[]{:S(2)}, u32[]{:S(2)}) async-start(bf16[16,16,128]{2,1,0:T(8,128)(2,1)} %bitcast.3), calls=%async_computation.1 | async-start | bytes 131072 | tf_op jit(solution)/shard_map/all_to_all | solution.py:121
  188.7 14.7 %copy-start.1 = (bf16[512,1024]{1,0:T(8,128)(2,1)S(1)}, bf16[512,1024]{1,0:T(8,128)(2,1)}, u32[]{:S(2)}) copy-start(bf16[512,1024]{1,0:T(8,128)(2,1)} %param.14) | copy-start | bytes 3145732
  197.7 13.1 %all-to-all-start = ((bf16[16,16,512]{2,1,0:T(8,128)(2,1)}), bf16[16,16,512]{2,1,0:T(8,128)(2,1)S(1)}, u32[]{:S(2)}, u32[]{:S(2)}) async-start(bf16[16,16,512]{2,1,0:T(8,128)(2,1)} %convert_element_type.63), calls=%async_computation | async-start | bytes 524288 | tf_op jit(solution)/shard_map/all_to_all | solution.py:120
  214.7 5.3 %copy-start.2 = (s32[256]{0:T(256)S(1)}, s32[256]{0:T(256)}, u32[]{:S(2)}) copy-start(s32[256]{0:T(256)} %param.17) | copy-start | bytes 3076
  214.7 98.7 %all-to-all-start.3 = ((bf16[8,512,1024]{1,2,0:T(8,128)(2,1)}), bf16[8,512,1024]{1,2,0:T(8,128)(2,1)}, u32[]{:S(2)}, u32[]{:S(2)}) async-start(bf16[8,512,1024]{1,2,0:T(8,128)(2,1)} %stack.2), calls=%async_computation.3 | async-start | bytes 16777216 | tf_op jit(solution)/shard_map/all_to_all | solution.py:130
  219.8 208.9 %reduce-scatter.2.cloned.1.call-start = ((), (), s32[]{:S(2)}) async-start(), calls=%async_computation.8 | async-start | bytes 8912896 | tf_op jit(solution)/shard_map/reduce_scatter | solution.py:134
  333.7 95.1 %copy-start = (bf16[256,512]{1,0:T(8,128)(2,1)S(1)}, bf16[256,512]{1,0:T(8,128)(2,1)}, u32[]{:S(2)}) copy-start(bf16[256,512]{1,0:T(8,128)(2,1)} %param.9) | copy-start | bytes 786436
  430.5 11.2 %all-to-all-start.4 = ((f32[16,1,256]{2,1,0:T(1,128)}), f32[16,1,256]{2,1,0:T(1,128)S(1)}, u32[]{:S(2)}, u32[]{:S(2)}) async-start(f32[16,1,256]{2,1,0:T(1,128)} %broadcast_in_dim.12), calls=%async_computation.5 | async-start | bytes 32768 | tf_op jit(solution)/shard_map/all_to_all | solution.py:21
Sparse Core Ops, SparseCore 0:
  9.6 40.6 all-gather.2
  52.6 124.6 all-gather.4
  333.8 94.8 reduce-scatter.1
